TPU v7x, 256 devices: a whole 4x4x8 slice. The times are simulated.
256 devices in a mesh: rows: 32 (over y, x, core), rhs: 8 (over z).
Axes of the slice: x: 4, y: 4, z: 8, core: 2. Of those that a mesh axis runs over, the one named last changes fastest.
Arguments:
- sources: bfloat16 [131072, 4096], P('rows', 'rhs'), may hold values from -6 to 6
- near_blocks: bfloat16 [512, 3, 256, 256], P('rows'), may hold values from -0.21875 to 0.21875
- near_list: int32 [512, 3], P('rows'), may hold values from 0 to 511, as said below
- source_basis: bfloat16 [512, 256, 32], P('rows'), may hold values from -0.375 to 0.375
- target_basis: bfloat16 [512, 256, 32], P('rows'), may hold values from -0.375 to 0.375
- transfer_fine: bfloat16 [896, 32, 32], P('rows'), may hold values from -0.875 to 0.875
- transfer_coarse: bfloat16 [128, 32, 32], P('rhs'), may hold values from -0.875 to 0.875
- couple_fine: bfloat16 [896, 3, 32, 32], P('rows'), may hold values from -0.625 to 0.625
- couple_coarse: bfloat16 [128, 3, 32, 32], P('rhs'), may hold values from -0.625 to 0.625
- far_fine: int32 [896, 3], P('rows'), may hold values from 0 to 511, as said below
- far_coarse: int32 [128, 3], replicated, may hold values from -1 to 63, as said below
Outputs:
- potentials: bfloat16 [131072, 4096], P('rows', 'rhs')
Inputs may be any that keep to these rules, and one draw needn't show every extreme that they name: `near_list`: row t lists the leaf clusters t - 1, t and t + 1 modulo 512 in some order. `far_fine`: row d * 28 + o + i belongs to cluster d * m + i of the level with n = m * 32 clusters, where (o, m) is (0, 16), (16, 8) or (24, 4). It lists, in some order, the three clusters of that level that are children of the cyclic neighbours of the cluster's parent and not cyclic neighbours of the cluster: for cluster j with parent p = j // 2, the clusters 2p - 2, 2p + 2, 2p + 3 if j is even and 2p - 2, 2p - 1, 2p + 3 if j is odd, modulo n. `far_coarse`: row n + j for n = 8, 16, ..., 64 lists, in some order, the three far clusters of cluster j of the level with n clusters by the rule of far_fine. Row 4 + j holds (j + 2) modulo 4 in slot 0 and -1 in slots 1 and 2. Rows 0 to 3 hold -1.
All inputs are finite; a program needn't handle non-finite values.
Results may differ from a plain program's by a relative error of at most 0.012.
Values may be sent and summed in bfloat16 or wider, within the bound.
A program may use at most 128 MiB of HBM per device.

v0:
```python
import jax
import jax.numpy as jnp
from jax import lax
from jax.sharding import PartitionSpec as P


def padded_2(cells, sides, width):
    for axis, dim in sides:
        count = lax.axis_size(axis)
        head = lax.slice_in_dim(cells, 0, width, axis=dim)
        tail = lax.slice_in_dim(cells, cells.shape[dim] - width, cells.shape[dim], axis=dim)
        cells = jnp.concatenate(
            [
                lax.ppermute(tail, axis, [(i, (i + 1) % count) for i in range(count)]),
                cells,
                lax.ppermute(head, axis, [((i + 1) % count, i) for i in range(count)]),
            ],
            axis=dim,
        )
    return cells


def from_everyone(shard, axis):
    copies = jnp.broadcast_to(shard, (lax.axis_size(axis), *shard.shape))
    return lax.all_to_all(copies, axis, split_axis=0, concat_axis=0, tiled=True)


def joined_along(pieces, dim):
    pieces = jnp.moveaxis(pieces, 0, dim)
    dims = pieces.shape
    return pieces.reshape(*dims[:dim], dims[dim] * dims[dim + 1], *dims[dim + 2 :])


def gather_directly(shard, axis, dim):
    pieces = from_everyone(shard, axis)
    return joined_along(pieces, dim)


def sent_together(arrays, axis, dim, along):
    columns = [a.reshape(*a.shape[:along], -1) for a in arrays]
    both = jnp.concatenate(columns, axis=along)
    whole, at, finished = (gather_directly(both, axis, dim), 0, [])
    for a, column in zip(arrays, columns):
        slab = whole[..., at : at + column.shape[along]]
        finished.append(slab.reshape(*slab.shape[:along], *a.shape[along:]))
        at += column.shape[along]
    return tuple(finished)


def couple_masked(moments, blocks, partners):
    valid = partners >= 0
    picked = moments[jnp.maximum(partners, 0)]
    picked = jnp.where(valid[:, :, None, None], picked, jnp.zeros_like(picked))
    return jnp.einsum("nsab,nsbr->nar", blocks, picked, preferred_element_type=jnp.float32)


def routed_blocks(blocks, offset, wanted):
    chosen = jnp.zeros_like(blocks[:, 0])
    for slot in range(3):
        match = (offset[:, slot] == wanted)[:, None, None]
        chosen = jnp.where(match, blocks[:, slot], chosen)
    return chosen


def couple_window(moments, blocks, partners, position, row_count):
    clusters = moments.shape[0]
    level_size = clusters * row_count
    window = padded_2(moments, (("rows", 0),), 3)
    targets = position * clusters + jnp.arange(clusters, dtype=jnp.int32)
    offset = (partners - targets[:, None] + level_size // 2) % level_size - level_size // 2
    coupled = jnp.zeros((clusters, moments.shape[1], moments.shape[2]), jnp.float32)
    for wanted in (-3, -2, 2, 3):
        chosen = routed_blocks(blocks, offset, wanted)
        shifted = window[3 + wanted : 3 + wanted + clusters]
        coupled = coupled + jnp.einsum(
            "nab,nbr->nar", chosen, shifted, preferred_element_type=jnp.float32
        )
    return coupled


def lift(moments, transfer):
    clusters, rank, width = moments.shape
    product = jnp.einsum("nab,nar->nbr", transfer, moments, preferred_element_type=jnp.float32)
    return product.reshape(clusters // 2, 2, rank, width).sum(axis=1).astype(jnp.bfloat16)


def lower(parent, transfer, coupled):
    spread = jnp.repeat(parent, 2, axis=0)
    carried = jnp.einsum("nab,nbr->nar", transfer, spread, preferred_element_type=jnp.float32)
    return (coupled + carried).astype(jnp.bfloat16)


def coarse_pass(moments, transfer_all, couple_all, far_all):
    clusters = moments.shape[0]
    depth = clusters.bit_length() - 3
    upward = [moments]
    for step in range(depth):
        moments = lift(moments, transfer_all[clusters : 2 * clusters])
        clusters = clusters // 2
        upward.append(moments)
    downward = moments
    for step in range(depth + 1):
        coupled = couple_masked(
            upward[depth - step],
            couple_all[clusters : 2 * clusters],
            far_all[clusters : 2 * clusters],
        )
        if step == 0:
            downward = coupled.astype(jnp.bfloat16)
        else:
            downward = lower(downward, transfer_all[clusters : 2 * clusters], coupled)
        clusters = clusters * 2
    return downward


def body(
    sources,
    near_blocks,
    near_list,
    source_basis,
    target_basis,
    transfer_fine,
    transfer_coarse,
    couple_fine,
    couple_coarse,
    far_fine,
    far_coarse,
):
    count = near_blocks.shape[0]
    leaf = near_blocks.shape[2]
    width = sources.shape[1]
    row_count = lax.axis_size("rows")
    position = lax.axis_index("rows")
    all_leaves = count * row_count
    padded = padded_2(sources, (("rows", 0),), leaf)
    neighbours = padded.reshape(count + 2, leaf, width)
    targets = position * count + jnp.arange(count, dtype=jnp.int32)
    offset = (near_list - targets[:, None] + all_leaves // 2) % all_leaves - all_leaves // 2
    near_part = jnp.zeros((count, leaf, width), jnp.float32)
    for wanted in (-1, 0, 1):
        chosen = routed_blocks(near_blocks, offset, wanted)
        shifted = neighbours[1 + wanted : 1 + wanted + count]
        near_part = near_part + jnp.einsum(
            "npq,nqr->npr", chosen, shifted, preferred_element_type=jnp.float32
        )
    shaped = sources.reshape(count, leaf, width)
    moments = jnp.einsum(
        "npk,npr->nkr", source_basis, shaped, preferred_element_type=jnp.float32
    ).astype(jnp.bfloat16)
    level_counts = [count, count // 2, count // 4]
    firsts = [0, count, count + count // 2]
    upward = [moments]
    for level in range(3):
        moments = lift(moments, transfer_fine[firsts[level] : firsts[level] + level_counts[level]])
        upward.append(moments)
    tables = sent_together((transfer_coarse, couple_coarse), "rhs", 0, 1)
    columns = lax.all_to_all(moments, "rows", split_axis=2, concat_axis=0, tiled=True)
    result = coarse_pass(columns, tables[0], tables[1], far_coarse)
    parents = lax.all_to_all(result, "rows", split_axis=0, concat_axis=2, tiled=True)
    downward = parents
    for level in (2, 1, 0):
        first = firsts[level]
        last = first + level_counts[level]
        coupled = couple_window(
            upward[level], couple_fine[first:last], far_fine[first:last], position, row_count
        )
        downward = lower(downward, transfer_fine[first:last], coupled)
    far_part = jnp.einsum(
        "npk,nkr->npr", target_basis, downward, preferred_element_type=jnp.float32
    )
    return (far_part + near_part).astype(jnp.bfloat16).reshape(count * leaf, width)


def solution(mesh):
    in_specs = (
        P("rows", "rhs"),
        P("rows", None, None, None),
        P("rows", None),
        P("rows", None, None),
        P("rows", None, None),
        P("rows", None, None),
        P("rhs", None, None),
        P("rows", None, None, None),
        P("rhs", None, None, None),
        P("rows", None),
        P(),
    )
    out_specs = P("rows", "rhs")
    return jax.shard_map(body, mesh=mesh, in_specs=in_specs, out_specs=out_specs, check_vma=False)
```

profile of v0, /device:TPU:1, one launch (start us, length us, event | category | flops | bytes accessed | tf_op | source)
XLA Modules:
  0.0 168.6 jit_solution(6814324130455730087)
XLA Ops:
  0.1 3.2 %convolution_convert_fusion = bf16[16,32,512]{2,1,0:T(8,128)(2,1)S(1)} fusion(bf16[16,256,32]{1,2,0:T(8,128)(2,1)} %param.14, bf16[16,256,512]{2,1,0:T(8,128)(2,1)} %bitcast.431), kind=kOutput, calls=%fused_computation.51 | convolution fusion | flops 134479872 | bytes 4980736 | tf_op jit(solution)/shard_map/npk,npr->nkr/dot_general | solution.py:147
  3.9 2.6 %collective-permute-start = (bf16[3,32,512]{2,1,0:T(8,128)(2,1)}, bf16[3,32,512]{2,1,0:T(8,128)(2,1)S(1)}, u32[]{:S(2)}, u32[]{:S(2)}) collective-permute-start(bf16[3,32,512]{2,1,0:T(8,128)(2,1)} %get-tuple-element.9), channel_id=1, source_target_pairs={{0,8},{8,16},{16,24},{24,32},{32,40},{40,48},{48,56},{56,64},{64,7... | collective-permute-start | bytes 294920 | tf_op jit(solution)/shard_map/ppermute | solution.py:14
  9.0 8.5 %all-to-all-start.1 = ((bf16[32,2,512]{2,1,0:T(2,128)(2,1)}), bf16[32,2,512]{2,1,0:T(2,128)(2,1)S(1)}, u32[]{:S(2)}, u32[]{:S(2)}) async-start(bf16[32,2,512]{2,1,0:T(2,128)(2,1)} %reshape.478), calls=%async_computation.1 | async-start | bytes 131072 | tf_op jit(solution)/shard_map/all_to_all | solution.py:157
  18.2 1.6 collective-permute-start.4
  20.5 3.8 %collective-permute-start.3 = (bf16[3,32,512]{2,1,0:T(8,128)(2,1)S(1)}, bf16[3,32,512]{2,1,0:T(8,128)(2,1)S(1)}, u32[]{:S(2)}, u32[]{:S(2)}) collective-permute-start(bf16[3,32,512]{2,1,0:T(8,128)(2,1)S(1)} %get-tuple-element.12), channel_id=1, source_target_pairs={{8,0},{16,8},{24,16},{32,24},{40,32},{48,40},{56,48},{64,56},{72,6... | collective-permute-start | bytes 294920 | tf_op jit(solution)/shard_map/ppermute | solution.py:16
  25.0 1.8 %fusion.297 = (bf16[256,512]{1,0:T(8,128)(2,1)}, bf16[256,512]{1,0:T(8,128)(2,1)S(1)}) fusion(bf16[4096,512]{1,0:T(8,128)(2,1)} %param.11), kind=kLoop, calls=%fused_computation.404 | loop fusion | bytes 1048576 | tf_op jit(solution)/shard_map/slice | solution.py:10
  36.8 8.7 %fusion.7 = f32[16,256,512]{2,1,0:T(8,128)} fusion(bf16[16,256,512]{2,1,0:T(8,128)(2,1)} %bitcast.432, pred[16]{0:T(512)(128)(4,1)S(1)} %get-tuple-element.19, pred[16]{0:T(512)(128)(4,1)S(1)} %get-tuple-element.17, pred[16]{0:T(512)(128)(4,1)S(1)} %get-tuple-element.16, bf16[16,3,256,256]{3,2,1,0:T(8,128)(2,1)} %param.12), kind=kOutput, calls=%fused_computation.17 | convolution fusion | flops 1076887552 | bytes 18874416 | tf_op jit(solution)/shard_map/npq,nqr->npr/dot_general | solution.py:143
  45.5 1.1 broadcast_in_dim.421
  46.6 6.8 %all-to-all-start = ((bf16[8,16,4096]{2,1,0:T(8,128)(2,1)}), bf16[8,16,4096]{2,1,0:T(8,128)(2,1)}, u32[]{:S(2)}, u32[]{:S(2)}) async-start(bf16[8,16,4096]{2,1,0:T(8,128)(2,1)} %broadcast_in_dim.421), calls=%async_computation | async-start | bytes 2097152 | tf_op jit(solution)/shard_map/all_to_all | solution.py:25
  53.6 1.6 gather_fusion
  55.4 2.0 %fusion.80 = f32[8,32,512]{2,1,0:T(8,128)} fusion(bf16[3,32,512]{2,1,0:T(8,128)(2,1)S(1)} %collective-permute-done.3, bf16[8,32,512]{2,1,0:T(8,128)(2,1)S(1)} %bitcast_reduce_fusion, pred[8]{0:T(512)(128)(4,1)S(1)} %get-tuple-element.45, pred[8]{0:T(512)(128)(4,1)S(1)} %get-tuple-element.42, pred[8]{0:T(512)(128)(4,1)S(1)} %get-tuple-element.39, ...), kind=kOutput, calls=%fused_computation.111 | convolution fusion | flops 8544256 | bytes 1081368 | tf_op jit(solution)/shard_map/nab,nbr->nar/dot_general | solution.py:75
  58.0 1.6 fusion.68
  59.7 2.0 %fusion.76 = f32[8,32,512]{2,1,0:T(8,128)} fusion(bf16[8,32,512]{2,1,0:T(8,128)(2,1)S(1)} %bitcast_reduce_fusion, bf16[3,32,512]{2,1,0:T(8,128)(2,1)S(1)} %collective-permute-done.3, pred[8]{0:T(512)(128)(4,1)S(1)} %copy-done.42, pred[8]{0:T(512)(128)(4,1)S(1)} %copy-done.41, pred[8]{0:T(512)(128)(4,1)S(1)} %copy-done.40, bf16[28,3,32,32]{3,2,1,0:T(8,128)(2,1)} %param.18), kind=kOutput, calls=%fused_computation.108 | convolution fusion | flops 8544256 | bytes 1081368 | tf_op jit(solution)/shard_map/nab,nbr->nar/dot_general | solution.py:75
  61.7 1.1 collective-permute-start.6
  62.8 2.0 %fusion.82 = f32[8,32,512]{2,1,0:T(8,128)} fusion(bf16[8,32,512]{2,1,0:T(8,128)(2,1)S(1)} %bitcast_reduce_fusion, bf16[3,32,512]{2,1,0:T(8,128)(2,1)S(1)} %collective-permute-done.2, pred[8]{0:T(512)(128)(4,1)S(1)} %get-tuple-element.43, pred[8]{0:T(512)(128)(4,1)S(1)} %get-tuple-element.40, pred[8]{0:T(512)(128)(4,1)S(1)} %get-tuple-element.37, ...), kind=kOutput, calls=%fused_computation.114 | convolution fusion | flops 8544256 | bytes 1081368 | tf_op jit(solution)/shard_map/nab,nbr->nar/dot_general | solution.py:75
  64.8 1.7 %fusion.92 = f32[4,32,512]{2,1,0:T(8,128)} fusion(bf16[3,32,512]{2,1,0:T(8,128)(2,1)S(1)} %collective-permute-done.5, bf16[4,32,512]{2,1,0:T(8,128)(2,1)S(1)} %bitcast_reduce_fusion.1, pred[4]{0:T(512)(128)(4,1)S(1)} %get-tuple-element.57, pred[4]{0:T(512)(128)(4,1)S(1)} %get-tuple-element.54, pred[4]{0:T(512)(128)(4,1)S(1)} %get-tuple-element.51, ...), kind=kOutput, calls=%fused_computation.129 | convolution fusion | flops 4272128 | bytes 589836 | tf_op jit(solution)/shard_map/nab,nbr->nar/dot_general | solution.py:75
  66.5 2.4 %fusion.63 = f32[16,32,512]{2,1,0:T(8,128)} fusion(bf16[16,32,512]{2,1,0:T(8,128)(2,1)S(1)} %convolution_convert_fusion, bf16[3,32,512]{2,1,0:T(8,128)(2,1)} %copy-done.15, pred[16]{0:T(512)(128)(4,1)S(1)} %copy-done.45, pred[16]{0:T(512)(128)(4,1)S(1)} %copy-done.44, pred[16]{0:T(512)(128)(4,1)S(1)} %copy-done.43, bf16[28,3,32,32]{3,2,1,0:T(8,128)(2,1)} %param.18), kind=kOutput, calls=%fused_computation.90 | convolution fusion | flops 17088512 | bytes 2064432 | tf_op jit(solution)/shard_map/nab,nbr->nar/dot_general | solution.py:75
  68.9 1.7 %fusion.88 = f32[4,32,512]{2,1,0:T(8,128)} fusion(bf16[4,32,512]{2,1,0:T(8,128)(2,1)S(1)} %bitcast_reduce_fusion.1, bf16[3,32,512]{2,1,0:T(8,128)(2,1)S(1)} %collective-permute-done.5, pred[4]{0:T(512)(128)(4,1)S(1)} %get-tuple-element.56, pred[4]{0:T(512)(128)(4,1)S(1)} %get-tuple-element.53, pred[4]{0:T(512)(128)(4,1)S(1)} %get-tuple-element.50, ...), kind=kOutput, calls=%fused_computation.126 | convolution fusion | flops 4272128 | bytes 589836 | tf_op jit(solution)/shard_map/nab,nbr->nar/dot_general | solution.py:75
  70.6 1.8 %fusion.94 = f32[4,32,512]{2,1,0:T(8,128)} fusion(bf16[4,32,512]{2,1,0:T(8,128)(2,1)S(1)} %bitcast_reduce_fusion.1, bf16[3,32,512]{2,1,0:T(8,128)(2,1)S(1)} %collective-permute-done.4, pred[4]{0:T(512)(128)(4,1)S(1)} %get-tuple-element.55, pred[4]{0:T(512)(128)(4,1)S(1)} %get-tuple-element.52, pred[4]{0:T(512)(128)(4,1)S(1)} %get-tuple-element.49, ...), kind=kOutput, calls=%fused_computation.132 | convolution fusion | flops 4272128 | bytes 589836 | tf_op jit(solution)/shard_map/nab,nbr->nar/dot_general | solution.py:75
  72.5 2.4 %fusion.70 = f32[16,32,512]{2,1,0:T(8,128)} fusion(bf16[16,32,512]{2,1,0:T(8,128)(2,1)S(1)} %convolution_convert_fusion, bf16[3,32,512]{2,1,0:T(8,128)(2,1)S(1)} %collective-permute-done, pred[16]{0:T(512)(128)(4,1)S(1)} %copy-done.30, pred[16]{0:T(512)(128)(4,1)S(1)} %copy-done.29, pred[16]{0:T(512)(128)(4,1)S(1)} %copy-done.28, ...), kind=kOutput, calls=%fused_computation.96 | convolution fusion | flops 17088512 | bytes 2064432 | tf_op jit(solution)/shard_map/nab,nbr->nar/dot_general | solution.py:75
  74.9 3.6 %pad_maximum_fusion = (bf16[4096,512]{1,0:T(8,128)(2,1)}, bf16[4096,512]{1,0:T(8,128)(2,1)}) fusion(bf16[256,512]{1,0:T(8,128)(2,1)S(1)} %collective-permute-done.7, bf16[4096,512]{1,0:T(8,128)(2,1)S(1)} %copy-done.1, bf16[256,512]{1,0:T(8,128)(2,1)S(1)} %collective-permute-done.6), kind=kLoop, calls=%fused_computation.7 | loop fusion | flops 16777216 | bytes 13107200 | tf_op jit(solution)/shard_map/concatenate | solution.py:12
  78.5 4.2 %all-to-all-done = bf16[8,16,4096]{2,1,0:T(8,128)(2,1)} async-done(((bf16[8,16,4096]{2,1,0:T(8,128)(2,1)}), bf16[8,16,4096]{2,1,0:T(8,128)(2,1)}, u32[]{:S(2)}, u32[]{:S(2)}) %all-to-all-start) | async-done | bytes 1048608 | tf_op jit(solution)/shard_map/all_to_all | solution.py:25
  86.6 1.5 slice.452
  89.1 1.6 slice.450
  90.7 1.8 %slice.448 = bf16[64,3072]{1,0:T(8,128)(2,1)} slice(bf16[128,4096]{1,0:T(8,128)(2,1)} %bitcast.50), slice={[64:128], [1024:4096]} | slice | bytes 786432 | tf_op jit(solution)/shard_map/slice | solution.py:105
  96.0 1.7 %copy.129 = bf16[64,32,32]{2,1,0:T(8,128)(2,1)S(1)} copy(bf16[64,32,32]{0,2,1:T(8,128)(2,1)} %bitcast.441) | data formatting | bytes 262144 | tf_op jit(solution)/shard_map/slice | solution.py:111
  99.4 1.3 gather_fusion.3
  100.7 1.4 gather_fusion.2
  102.1 1.5 gather_fusion.1
  103.6 2.0 %slice.396 = bf16[16,3,32,32]{3,2,1,0:T(8,128)(2,1)} reshape(bf16[16,3072]{1,0:T(8,128)(2,1)} %slice.452) | data formatting | bytes 196608 | tf_op jit(solution)/shard_map/slice | solution.py:105
  105.6 2.2 %copy.111 = bf16[64,3072]{0,1:T(8,128)(2,1)} copy(bf16[64,3072]{1,0:T(8,128)(2,1)} %slice.448) | data formatting | bytes 786432 | tf_op jit(solution)/shard_map/slice | solution.py:105
  107.9 2.4 %slice.391 = bf16[32,3,32,32]{3,2,1,0:T(8,128)(2,1)} reshape(bf16[32,3072]{1,0:T(8,128)(2,1)} %slice.450) | data formatting | bytes 393216 | tf_op jit(solution)/shard_map/slice | solution.py:105
  110.2 3.1 %copy.118 = bf16[64,3,32,32]{3,2,1,0:T(8,128)(2,1)} copy(bf16[64,3,32,32]{0,3,2,1:T(8,128)(2,1)} %bitcast.438) | data formatting | bytes 786432 | tf_op jit(solution)/shard_map/slice | solution.py:105
  113.3 1.3 gather_fusion.4
  114.6 1.2 fusion.56
  115.8 1.2 convolution_bitcast_fusion.6
  117.1 1.0 fusion.55
  118.1 1.4 convolution_bitcast_fusion.5
  119.8 1.6 convolution_bitcast_fusion.4
  121.7 1.9 %convolution_bitcast_fusion.2 = f32[64,32,16]{1,2,0:T(8,128)S(1)} fusion(bf16[64,3,32,32]{3,2,1,0:T(8,128)(2,1)S(1)} %copy-done.3, bf16[64,3,32,16]{2,3,1,0:T(8,128)(2,1)} %bitcast.437, pred[64,3]{1,0:T(8,128)(4,1)S(1)} %copy-done.17), kind=kOutput, calls=%fused_computation.53 | convolution fusion | flops 6389760 | bytes 721088 | tf_op jit(solution)/shard_map/nsab,nsbr->nar/dot_general | solution.py:54
  124.8 6.3 %all-to-all-start.2 = ((bf16[32,2,512]{2,1,0:T(2,128)(2,1)}), bf16[32,2,512]{2,1,0:T(2,128)(2,1)S(1)}, u32[]{:S(2)}, u32[]{:S(2)}) async-start(bf16[32,2,512]{2,1,0:T(2,128)(2,1)} %reshape.480), calls=%async_computation.2 | async-start | bytes 131072 | tf_op jit(solution)/shard_map/all_to_all | solution.py:159
  131.2 8.6 %fusion.3 = f32[16,256,512]{2,1,0:T(8,128)} fusion(bf16[16,256,512]{2,1,0:T(8,128)(2,1)} %bitcast.436, pred[16]{0:T(512)(128)(4,1)S(1)} %copy-done.37, pred[16]{0:T(512)(128)(4,1)S(1)} %copy-done.38, pred[16]{0:T(512)(128)(4,1)S(1)} %copy-done.39, bf16[16,3,256,256]{3,2,1,0:T(8,128)(2,1)} %param.12), kind=kOutput, calls=%fused_computation.14 | convolution fusion | flops 1076887552 | bytes 18874416 | tf_op jit(solution)/shard_map/npq,nqr->npr/dot_general | solution.py:143
  141.2 1.4 fusion.53
  142.7 1.0 convolution_bitcast_fusion.1
  143.8 1.6 fusion.48
  145.5 1.2 convolution_bitcast_fusion
  146.7 6.6 %fusion.46 = f32[16,512,256]{1,2,0:T(8,128)} fusion(bf16[16,256,32]{1,2,0:T(8,128)(2,1)S(1)} %copy-done, f32[16,32,512]{2,1,0:T(8,128)S(1)} %convolution_bitcast_fusion, f32[16,32,512]{2,1,0:T(8,128)S(1)} %fusion.68, f32[16,32,512]{2,1,0:T(8,128)} %fusion.63, f32[16,32,512]{2,1,0:T(8,128)} %fusion.70, bf16[3,32,512]{2,1,0:T(8,128)(2,1)S(1)} %copy-done.7, ...), kind=kOutput, calls=%fused_computation.58 | convolution fusion | flops 152616960 | bytes 13860912 | tf_op jit(solution)/shard_map/npk,nkr->npr/dot_general | solution.py:168
  153.3 15.3 %fusion = bf16[16,256,512]{2,1,0:T(8,128)(2,1)} fusion(f32[16,512,256]{1,2,0:T(8,128)} %fusion.46, f32[16,256,512]{2,1,0:T(8,128)} %fusion.3, f32[16,256,512]{2,1,0:T(8,128)} %fusion.7, bf16[16,256,512]{2,1,0:T(8,128)(2,1)} %bitcast.435, pred[16]{0:T(512)(128)(4,1)S(1)} %copy-done.36, pred[16]{0:T(512)(128)(4,1)S(1)} %copy-done.35, ...), kind=kOutput, calls=%fused_computation.6 | convolution fusion | flops 1085276160 | bytes 39845936 | tf_op jit(solution)/shard_map/npq,nqr->npr/dot_general | solution.py:143
  (191 shorter events, 29.5 us)
Async XLA Ops:
  0.0 146.6 %copy-start = (bf16[16,256,32]{1,2,0:T(8,128)(2,1)S(1)}, bf16[16,256,32]{1,2,0:T(8,128)(2,1)}, u32[]{:S(2)}) copy-start(bf16[16,256,32]{1,2,0:T(8,128)(2,1)} %param.15) | copy-start | bytes 786436
  0.0 7.1 %copy-start.5 = (bf16[28,32,32]{2,1,0:T(8,128)(2,1)S(1)}, bf16[28,32,32]{2,1,0:T(8,128)(2,1)}, u32[]{:S(2)}) copy-start(bf16[28,32,32]{2,1,0:T(8,128)(2,1)} %param.16) | copy-start | bytes 172036
  0.0 24.3 %copy-start.13 = (s32[128,3]{0,1:T(4,128)S(1)}, s32[128,3]{0,1:T(4,128)}, u32[]{:S(2)}) copy-start(s32[128,3]{0,1:T(4,128)} %param.21) | copy-start | bytes 4612
  0.0 28.8 %copy-start.16 = (s32[28,3]{0,1:T(4,128)S(1)}, s32[28,3]{0,1:T(4,128)}, u32[]{:S(2)}) copy-start(s32[28,3]{0,1:T(4,128)} %param.20) | copy-start | bytes 1012
  0.0 31.2 %copy-start.24 = (s32[16,3]{0,1:T(4,128)S(1)}, s32[16,3]{0,1:T(4,128)}, u32[]{:S(2)}) copy-start(s32[16,3]{0,1:T(4,128)} %param.13) | copy-start | bytes 580
  0.0 36.1 %copy-start.14 = (bf16[16,32,32]{2,1,0:T(8,128)(2,1)S(1)}, bf16[16,32,32]{2,1,0:T(8,128)(2,1)}, u32[]{:S(2)}) copy-start(bf16[16,32,32]{2,1,0:T(8,128)(2,1)} %param.17) | copy-start | bytes 98308
  0.0 36.3 %copy-start.12 = (bf16[16,3,32,32]{3,2,1,0:T(8,128)(2,1)S(1)}, bf16[16,3,32,32]{3,2,1,0:T(8,128)(2,1)}, u32[]{:S(2)}) copy-start(bf16[16,3,32,32]{3,2,1,0:T(8,128)(2,1)} %param.19) | copy-start | bytes 294916
  3.9 68.6 %collective-permute-start = (bf16[3,32,512]{2,1,0:T(8,128)(2,1)}, bf16[3,32,512]{2,1,0:T(8,128)(2,1)S(1)}, u32[]{:S(2)}, u32[]{:S(2)}) collective-permute-start(bf16[3,32,512]{2,1,0:T(8,128)(2,1)} %get-tuple-element.9), channel_id=1, source_target_pairs={{0,8},{8,16},{16,24},{24,32},{32,40},{40,48},{48,56},{56,64},{64,7... | collective-permute-start | bytes 294920 | tf_op jit(solution)/shard_map/ppermute | solution.py:14
  6.5 50.9 %collective-permute-start.1 = (bf16[3,32,512]{2,1,0:T(8,128)(2,1)S(1)}, bf16[3,32,512]{2,1,0:T(8,128)(2,1)S(1)}, u32[]{:S(2)}, u32[]{:S(2)}) collective-permute-start(bf16[3,32,512]{2,1,0:T(8,128)(2,1)S(1)} %get-tuple-element.10), channel_id=1, source_target_pairs={{8,0},{16,8},{24,16},{32,24},{40,32},{48,40},{56,48},{64,56},{72,6... | collective-permute-start | bytes 294920 | tf_op jit(solution)/shard_map/ppermute | solution.py:16
  9.0 36.5 %all-to-all-start.1 = ((bf16[32,2,512]{2,1,0:T(2,128)(2,1)}), bf16[32,2,512]{2,1,0:T(2,128)(2,1)S(1)}, u32[]{:S(2)}, u32[]{:S(2)}) async-start(bf16[32,2,512]{2,1,0:T(2,128)(2,1)} %reshape.478), calls=%async_computation.1 | async-start | bytes 131072 | tf_op jit(solution)/shard_map/all_to_all | solution.py:157
  18.2 52.4 %collective-permute-start.4 = (bf16[3,32,512]{2,1,0:T(8,128)(2,1)}, bf16[3,32,512]{2,1,0:T(8,128)(2,1)S(1)}, u32[]{:S(2)}, u32[]{:S(2)}) collective-permute-start(bf16[3,32,512]{2,1,0:T(8,128)(2,1)} %get-tuple-element.13), channel_id=1, source_target_pairs={{0,8},{8,16},{16,24},{24,32},{32,40},{40,48},{48,56},{56,64},{64,7... | collective-permute-start | bytes 294920 | tf_op jit(solution)/shard_map/ppermute | solution.py:14
  19.8 44.9 %collective-permute-start.5 = (bf16[3,32,512]{2,1,0:T(8,128)(2,1)}, bf16[3,32,512]{2,1,0:T(8,128)(2,1)S(1)}, u32[]{:S(2)}, u32[]{:S(2)}) collective-permute-start(bf16[3,32,512]{2,1,0:T(8,128)(2,1)} %get-tuple-element.14), channel_id=1, source_target_pairs={{8,0},{16,8},{24,16},{32,24},{40,32},{48,40},{56,48},{64,56},{72,6... | collective-permute-start | bytes 294920 | tf_op jit(solution)/shard_map/ppermute | solution.py:16
  20.5 34.8 %collective-permute-start.3 = (bf16[3,32,512]{2,1,0:T(8,128)(2,1)S(1)}, bf16[3,32,512]{2,1,0:T(8,128)(2,1)S(1)}, u32[]{:S(2)}, u32[]{:S(2)}) collective-permute-start(bf16[3,32,512]{2,1,0:T(8,128)(2,1)S(1)} %get-tuple-element.12), channel_id=1, source_target_pairs={{8,0},{16,8},{24,16},{32,24},{40,32},{48,40},{56,48},{64,56},{72,6... | collective-permute-start | bytes 294920 | tf_op jit(solution)/shard_map/ppermute | solution.py:16
  45.5 12.6 %copy-start.31 = (pred[16]{0:T(512)(128)(4,1)S(1)}, pred[16]{0:T(512)(128)(4,1)}, u32[]{:S(2)}) copy-start(pred[16]{0:T(512)(128)(4,1)} %get-tuple-element.27) | copy-start | bytes 52
  45.5 12.6 %copy-start.32 = (pred[16]{0:T(512)(128)(4,1)S(1)}, pred[16]{0:T(512)(128)(4,1)}, u32[]{:S(2)}) copy-start(pred[16]{0:T(512)(128)(4,1)} %get-tuple-element.30) | copy-start | bytes 52
  45.5 12.6 %copy-start.33 = (pred[16]{0:T(512)(128)(4,1)S(1)}, pred[16]{0:T(512)(128)(4,1)}, u32[]{:S(2)}) copy-start(pred[16]{0:T(512)(128)(4,1)} %get-tuple-element.33) | copy-start | bytes 52
  46.6 13.1 %copy-start.40 = (pred[8]{0:T(512)(128)(4,1)S(1)}, pred[8]{0:T(512)(128)(4,1)}, u32[]{:S(2)}) copy-start(pred[8]{0:T(512)(128)(4,1)} %get-tuple-element.38) | copy-start | bytes 28
  46.6 13.1 %copy-start.41 = (pred[8]{0:T(512)(128)(4,1)S(1)}, pred[8]{0:T(512)(128)(4,1)}, u32[]{:S(2)}) copy-start(pred[8]{0:T(512)(128)(4,1)} %get-tuple-element.41) | copy-start | bytes 28
  46.6 13.1 %copy-start.42 = (pred[8]{0:T(512)(128)(4,1)S(1)}, pred[8]{0:T(512)(128)(4,1)}, u32[]{:S(2)}) copy-start(pred[8]{0:T(512)(128)(4,1)} %get-tuple-element.44) | copy-start | bytes 28
  46.6 36.1 %all-to-all-start = ((bf16[8,16,4096]{2,1,0:T(8,128)(2,1)}), bf16[8,16,4096]{2,1,0:T(8,128)(2,1)}, u32[]{:S(2)}, u32[]{:S(2)}) async-start(bf16[8,16,4096]{2,1,0:T(8,128)(2,1)} %broadcast_in_dim.421), calls=%async_computation | async-start | bytes 2097152 | tf_op jit(solution)/shard_map/all_to_all | solution.py:25
  53.6 12.9 %copy-start.43 = (pred[16]{0:T(512)(128)(4,1)S(1)}, pred[16]{0:T(512)(128)(4,1)}, u32[]{:S(2)}) copy-start(pred[16]{0:T(512)(128)(4,1)} %get-tuple-element.26) | copy-start | bytes 52
  53.6 12.9 %copy-start.44 = (pred[16]{0:T(512)(128)(4,1)S(1)}, pred[16]{0:T(512)(128)(4,1)}, u32[]{:S(2)}) copy-start(pred[16]{0:T(512)(128)(4,1)} %get-tuple-element.29) | copy-start | bytes 52
  53.6 12.9 %copy-start.45 = (pred[16]{0:T(512)(128)(4,1)S(1)}, pred[16]{0:T(512)(128)(4,1)}, u32[]{:S(2)}) copy-start(pred[16]{0:T(512)(128)(4,1)} %get-tuple-element.32) | copy-start | bytes 52
  55.3 17.2 %copy-start.28 = (pred[16]{0:T(512)(128)(4,1)S(1)}, pred[16]{0:T(512)(128)(4,1)}, u32[]{:S(2)}) copy-start(pred[16]{0:T(512)(128)(4,1)} %get-tuple-element.25) | copy-start | bytes 52
  55.3 17.2 %copy-start.29 = (pred[16]{0:T(512)(128)(4,1)S(1)}, pred[16]{0:T(512)(128)(4,1)}, u32[]{:S(2)}) copy-start(pred[16]{0:T(512)(128)(4,1)} %get-tuple-element.28) | copy-start | bytes 52
  55.3 17.2 %copy-start.30 = (pred[16]{0:T(512)(128)(4,1)S(1)}, pred[16]{0:T(512)(128)(4,1)}, u32[]{:S(2)}) copy-start(pred[16]{0:T(512)(128)(4,1)} %get-tuple-element.31) | copy-start | bytes 52
  55.3 6.4 %collective-permute-start.2 = (bf16[3,32,512]{2,1,0:T(8,128)(2,1)}, bf16[3,32,512]{2,1,0:T(8,128)(2,1)S(1)}, u32[]{:S(2)}, u32[]{:S(2)}) collective-permute-start(bf16[3,32,512]{2,1,0:T(8,128)(2,1)} %get-tuple-element.11), channel_id=1, source_target_pairs={{0,8},{8,16},{16,24},{24,32},{32,40},{40,48},{48,56},{56,64},{64,7... | collective-permute-start | bytes 294920 | tf_op jit(solution)/shard_map/ppermute | solution.py:14
  57.4 17.5 %collective-permute-start.7 = (bf16[256,512]{1,0:T(8,128)(2,1)}, bf16[256,512]{1,0:T(8,128)(2,1)S(1)}, u32[]{:S(2)}, u32[]{:S(2)}) collective-permute-start(bf16[256,512]{1,0:T(8,128)(2,1)} %get-tuple-element.7), channel_id=1, source_target_pairs={{8,0},{16,8},{24,16},{32,24},{40,32},{48,40},{56,48},{64,56},{72,6... | collective-permute-start | bytes 786440 | tf_op jit(solution)/shard_map/ppermute | solution.py:16
  58.0 16.8 %copy-start.1 = (bf16[4096,512]{1,0:T(8,128)(2,1)S(1)}, bf16[4096,512]{1,0:T(8,128)(2,1)}, u32[]{:S(2)}) copy-start(bf16[4096,512]{1,0:T(8,128)(2,1)} %param.11) | copy-start | bytes 12582916
  61.7 16.8 %copy-start.8 = (bf16[3,32,512]{2,1,0:T(8,128)(2,1)}, bf16[3,32,512]{2,1,0:T(8,128)(2,1)S(1)}, u32[]{:S(2)}) copy-start(bf16[3,32,512]{2,1,0:T(8,128)(2,1)S(1)} %collective-permute-done.2) | copy-start | bytes 294916
  61.7 13.2 %collective-permute-start.6 = (bf16[256,512]{1,0:T(8,128)(2,1)S(1)}, bf16[256,512]{1,0:T(8,128)(2,1)S(1)}, u32[]{:S(2)}, u32[]{:S(2)}) collective-permute-start(bf16[256,512]{1,0:T(8,128)(2,1)S(1)} %get-tuple-element.8), channel_id=1, source_target_pairs={{0,8},{8,16},{16,24},{24,32},{32,40},{40,48},{48,56},{56,64},{64,7... | collective-permute-start | bytes 786440 | tf_op jit(solution)/shard_map/ppermute | solution.py:14
  70.6 7.9 %copy-start.10 = (bf16[3,32,512]{2,1,0:T(8,128)(2,1)}, bf16[3,32,512]{2,1,0:T(8,128)(2,1)S(1)}, u32[]{:S(2)}) copy-start(bf16[3,32,512]{2,1,0:T(8,128)(2,1)S(1)} %collective-permute-done.4) | copy-start | bytes 294916
  103.6 16.1 %copy-start.4 = (bf16[96,32,16]{1,2,0:T(8,128)(2,1)S(1)}, bf16[96,32,16]{1,2,0:T(8,128)(2,1)}, u32[]{:S(2)}) copy-start(bf16[96,32,16]{1,2,0:T(8,128)(2,1)} %gather_fusion.1) | copy-start | bytes 294916
  114.6 7.0 %copy-start.3 = (bf16[64,3,32,32]{3,2,1,0:T(8,128)(2,1)S(1)}, bf16[64,3,32,32]{3,2,1,0:T(8,128)(2,1)}, u32[]{:S(2)}) copy-start(bf16[64,3,32,32]{3,2,1,0:T(8,128)(2,1)} %copy.118) | copy-start | bytes 1179652
  114.6 7.0 %copy-start.17 = (pred[64,3]{1,0:T(8,128)(4,1)S(1)}, pred[64,3]{1,0:T(8,128)(4,1)}, u32[]{:S(2)}) copy-start(pred[64,3]{1,0:T(8,128)(4,1)} %copy.112) | copy-start | bytes 580
  119.5 11.6 %copy-start.37 = (pred[16]{0:T(512)(128)(4,1)S(1)}, pred[16]{0:T(512)(128)(4,1)}, u32[]{:S(2)}) copy-start(pred[16]{0:T(512)(128)(4,1)} %get-tuple-element.21) | copy-start | bytes 52
  119.5 11.6 %copy-start.38 = (pred[16]{0:T(512)(128)(4,1)S(1)}, pred[16]{0:T(512)(128)(4,1)}, u32[]{:S(2)}) copy-start(pred[16]{0:T(512)(128)(4,1)} %get-tuple-element.22) | copy-start | bytes 52
  119.6 11.6 %copy-start.39 = (pred[16]{0:T(512)(128)(4,1)S(1)}, pred[16]{0:T(512)(128)(4,1)}, u32[]{:S(2)}) copy-start(pred[16]{0:T(512)(128)(4,1)} %get-tuple-element.23) | copy-start | bytes 52
  124.8 15.0 %all-to-all-start.2 = ((bf16[32,2,512]{2,1,0:T(2,128)(2,1)}), bf16[32,2,512]{2,1,0:T(2,128)(2,1)S(1)}, u32[]{:S(2)}, u32[]{:S(2)}) async-start(bf16[32,2,512]{2,1,0:T(2,128)(2,1)} %reshape.480), calls=%async_computation.2 | async-start | bytes 131072 | tf_op jit(solution)/shard_map/all_to_all | solution.py:159
  131.1 10.1 %copy-start.11 = (bf16[3,32,512]{2,1,0:T(8,128)(2,1)S(1)}, bf16[3,32,512]{2,1,0:T(8,128)(2,1)}, u32[]{:S(2)}) copy-start(bf16[3,32,512]{2,1,0:T(8,128)(2,1)} %copy-done.10) | copy-start | bytes 294916
  131.1 10.1 %copy-start.21 = (pred[4]{0:T(512)(128)(4,1)S(1)}, pred[4]{0:T(512)(128)(4,1)}, u32[]{:S(2)}) copy-start(pred[4]{0:T(512)(128)(4,1)} %get-tuple-element.48) | copy-start | bytes 16
  131.1 10.1 %copy-start.22 = (pred[4]{0:T(512)(128)(4,1)S(1)}, pred[4]{0:T(512)(128)(4,1)}, u32[]{:S(2)}) copy-start(pred[4]{0:T(512)(128)(4,1)} %get-tuple-element.58) | copy-start | bytes 16
  131.2 10.1 %copy-start.23 = (pred[4]{0:T(512)(128)(4,1)S(1)}, pred[4]{0:T(512)(128)(4,1)}, u32[]{:S(2)}) copy-start(pred[4]{0:T(512)(128)(4,1)} %get-tuple-element.59) | copy-start | bytes 16
  140.2 6.5 %copy-start.7 = (bf16[3,32,512]{2,1,0:T(8,128)(2,1)S(1)}, bf16[3,32,512]{2,1,0:T(8,128)(2,1)}, u32[]{:S(2)}) copy-start(bf16[3,32,512]{2,1,0:T(8,128)(2,1)} %copy-done.6) | copy-start | bytes 294916
  140.2 6.5 %copy-start.18 = (pred[16]{0:T(512)(128)(4,1)S(1)}, pred[16]{0:T(512)(128)(4,1)}, u32[]{:S(2)}) copy-start(pred[16]{0:T(512)(128)(4,1)} %get-tuple-element.24) | copy-start | bytes 52
  146.7 6.6 %copy-start.34 = (pred[16]{0:T(512)(128)(4,1)S(1)}, pred[16]{0:T(512)(128)(4,1)}, u32[]{:S(2)}) copy-start(pred[16]{0:T(512)(128)(4,1)} %get-tuple-element.15) | copy-start | bytes 52
  146.7 6.6 %copy-start.35 = (pred[16]{0:T(512)(128)(4,1)S(1)}, pred[16]{0:T(512)(128)(4,1)}, u32[]{:S(2)}) copy-start(pred[16]{0:T(512)(128)(4,1)} %get-tuple-element.18) | copy-start | bytes 52
  146.7 6.6 %copy-start.36 = (pred[16]{0:T(512)(128)(4,1)S(1)}, pred[16]{0:T(512)(128)(4,1)}, u32[]{:S(2)}) copy-start(pred[16]{0:T(512)(128)(4,1)} %get-tuple-element.20) | copy-start | bytes 52
  (9 other events, 39.3 us)
where the time goes:
time: 170 us; the launch traced here: 169 us
  matrix products  77.7 us (46%)
  local copies, waits for them, and re-layouts  44.4 us (26%)
  starting transfers between devices  32 us (19%)
  other arithmetic  9.4 us (6%)
  waiting for transfers between devices  4.21 us (2%)
    dot_general x3, matrix products, body(): jnp.einsum('npq,nqr->npr', chosen, shifted, preferred_element_type=jnp.fl...  32.6 us
    dot_general x11, matrix products, couple_window(): jnp.einsum('nab,nbr->nar', chosen, shifted, preferred_element_type=jnp.fl...  20.7 us
    slice x11, local copies, waits for them, and re-layouts, coarse_pass(): couple_all[clusters:2 * clusters]  17.8 us
    all_to_all x1, starting transfers between devices, body(): lax.all_to_all(moments, 'rows', split_axis=2, concat_axis=0, tiled=True)  8.54 us
    dot_general x5, matrix products, couple_masked(): jnp.einsum('nsab,nsbr->nar', blocks, picked, preferred_element_type=jnp.f...  7.33 us
    gather x5, local copies, waits for them, and re-layouts, couple_masked(): picked = moments[jnp.maximum(partners, 0)]  7.19 us
    slice x9, local copies, waits for them, and re-layouts, coarse_pass(): downward = lower(downward, transfer_all[clusters:2 * clusters], coupled)  6.86 us
    all_to_all x1, starting transfers between devices, from_everyone(): return lax.all_to_all(copies, axis, split_axis=0, concat_axis=0, tiled=True)  6.79 us
  transfers between devices with their start and end apart: 11, of which 1 were waited for; matrix products, arithmetic and copies ran while one was open for 34% of the time, Pallas kernels for 0%

commit v1 on v0

v1 whole, which is shorter than its diff:
```python
import jax
import jax.numpy as jnp
from jax import lax
from jax.experimental import pallas as pl
from jax.experimental.pallas import tpu as pltpu
from jax.sharding import PartitionSpec as P

MESH = pl.DeviceIdType.MESH
BF = jnp.bfloat16
F32 = jnp.float32
LEAF, RANK, LPD = 256, 32, 16
ROWS, CHIPS, DEEP = 32, 16, 8
WIDE, HALF = 512, 256
NEAR_FIRST = 8


def dot(a, b):
    return jnp.dot(a, b, preferred_element_type=F32)


def dot_t(a, b):
    return lax.dot_general(a, b, (((0,), (0,)), ((), ())), preferred_element_type=F32)


def dot_nt(a, b):
    return lax.dot_general(a, b, (((1,), (1,)), ((), ())), preferred_element_type=F32)


def iota(shape, dim):
    return lax.broadcasted_iota(jnp.int32, shape, dim)


def block_mask(shape, row_div, lane_div):
    return (iota(shape, 0) // row_div) % 4 == (iota(shape, 1) // lane_div) % 4


def routed(spread, fars, base, size):
    lanes = iota((RANK, 128), 1) // RANK
    total = jnp.zeros((RANK, 128), F32)
    for slot in range(3):
        place = (fars[slot] - base) & (size - 1)
        place = jnp.where(place < 2, place, place - 2)
        total = total + jnp.where(lanes == place, spread[slot * RANK : (slot + 1) * RANK], 0.0)
    return total


def tree_kernel(
    near_list, far_fine, far_coarse,
    sources, near_blocks, basis, transfer_fine, couple_fine, transfer_coarse, couple_coarse,
    moments_out, near_out,
    near, xs, nb, sb, tf, cf, tc, cc,
    eb, eu, s4, c512, c256, c128, c64, n64, n32, c16, c8, c4, f64,
    g512, g256, g128, g64, g32,
    se, ss, re64, re32, re16, re8, rs64, rs32, rs16, rs8, rs4,
    load_sem, store_sem, tab_send, tab_recv, halo_send, halo_recv, ring_send, ring_recv,
):
    r = lax.axis_index("rows")
    z = lax.axis_index("rhs")
    k = r // 2
    c = r % 2
    left, right = (r + ROWS - 1) % ROWS, (r + 1) % ROWS
    left2, right2 = (r + ROWS - 2) % ROWS, (r + 2) % ROWS
    partner = r + 1 - 2 * c
    other = (r + ROWS + 2 * c - 1) % ROWS
    z32, z64 = 2 + k // 8, 4 + k // 4

    barrier = pltpu.get_barrier_semaphore()

    def greet_rows(d, carry):
        there = ((k + d) % CHIPS) * 2 + c
        pl.semaphore_signal(barrier, inc=1, device_id={"rows": there}, device_id_type=MESH)
        return carry

    def greet_deep(d, carry):
        pl.semaphore_signal(barrier, inc=1, device_id={"rhs": (z + d) % DEEP}, device_id_type=MESH)
        return carry

    lax.fori_loop(1, DEEP, greet_deep, 0)
    lax.fori_loop(1, CHIPS, greet_rows, 0)
    for there in (partner, other):
        pl.semaphore_signal(barrier, inc=1, device_id={"rows": there}, device_id_type=MESH)

    loads = []

    def load(src, dst):
        copy = pltpu.make_async_copy(src, dst, load_sem.at[len(loads)])
        copy.start()
        loads.append(copy)
        return copy

    get_tc = load(transfer_coarse, tc)
    get_cc = load(couple_coarse, cc)
    get_tf = load(transfer_fine, tf)
    get_sb = load(basis, sb)
    chunk = 4 * LEAF
    get_xs = [
        load(sources.at[pl.ds(i * chunk, chunk)], xs.at[pl.ds(LEAF + i * chunk, chunk)]) for i in range(4)
    ]
    get_cf = load(couple_fine, cf)
    get_nb = load(near_blocks, nb)

    spread = jnp.where(iota((RANK, 128), 1) % RANK == iota((RANK, 128), 0), 1.0, 0.0).astype(BF)
    spread_t = jnp.where(iota((128, RANK), 0) % RANK == iota((128, RANK), 1), 1.0, 0.0).astype(BF)

    get_tc.wait()
    wide_e = dot(tc[...].reshape(LPD * RANK, RANK), spread)
    lane_block = iota((RANK, 128), 1) // RANK
    for group in range(2):
        for odd in range(2):
            total = jnp.zeros((RANK, 128), F32)
            for parent in range(4):
                row = (8 * group + 2 * parent + odd) * RANK
                total = total + jnp.where(lane_block == parent, wide_e[row : row + RANK], 0.0)
            se[group, odd * RANK : (odd + 1) * RANK, :] = total.astype(BF)
    get_cc.wait()
    for quarter in range(4):
        wide_s = dot(cc[4 * quarter : 4 * quarter + 4].reshape(4 * 3 * RANK, RANK), spread)
        first_size = {0: 4, 1: 4, 2: 8, 3: 8}[quarter]
        size = jnp.where(z >= 4, 64, jnp.where(z >= 2, 32, jnp.where(z == 1, 16, first_size)))
        for i in range(4):
            row = 4 * quarter + i
            mine = wide_s[i * 3 * RANK : (i + 1) * 3 * RANK]
            heap = z * LPD + row
            at = heap - size
            base = at - row % 2 - 2
            fars = [far_coarse[slot, heap] for slot in range(3)]
            block = routed(mine, fars, base, size)
            if quarter == 1:
                block = jnp.where(z == 0, mine[:RANK], block)
            ss[row * RANK : (row + 1) * RANK, :] = block.astype(BF)

    get_tf.wait()
    fine_e = tf[...].reshape(28 * RANK, RANK)
    eb[...] = jnp.where(block_mask((896, 128), 64, RANK), dot(fine_e, spread), 0.0).astype(BF)
    eu[...] = jnp.where(block_mask((128, 896), RANK, 64), dot_nt(spread_t, fine_e), 0.0).astype(BF)

    get_sb.wait()
    for i in range(4):
        get_xs[i].wait()
        for leaf in range(4 * i, 4 * i + 4):
            product = dot(sb[leaf], xs[LEAF * (leaf + 1) : LEAF * (leaf + 2), :])
            c512[64 + RANK * leaf : 64 + RANK * (leaf + 1), :] = product.astype(BF)

    pl.semaphore_wait(barrier, DEEP - 1 + CHIPS - 1 + 2)

    def table_copy(kind, src, dst, slot, d):
        return pltpu.make_async_remote_copy(
            src_ref=src, dst_ref=dst, send_sem=tab_send.at[slot, d], recv_sem=tab_recv.at[kind],
            device_id={"rhs": (z + d) % DEEP}, device_id_type=MESH,
        )

    e64_at = se.at[(k % 4) // 2]
    e32_at = se.at[(k % 8) // 4]
    rows64 = pl.ds(((4 * k) % LPD) * RANK, 4 * RANK)
    rows32 = pl.ds(((2 * k) % LPD) * RANK, 2 * RANK)
    rows16 = pl.ds(k * RANK, RANK)
    rows8 = pl.ds((8 + k // 2) * RANK, RANK)
    rows4 = pl.ds((4 + k // 4) * RANK, RANK)
    tables = [
        (z64, [(0, e64_at, re64), (1, ss.at[rows64], rs64)]),
        (z32, [(2, e32_at, re32), (3, ss.at[rows32], rs32)]),
        (1, [(4, se, re16), (5, ss.at[rows16], rs16)]),
        (0, [(6, se.at[1], re8), (7, ss.at[rows8], rs8), (8, ss.at[rows4], rs4)]),
    ]
    for owner, items in tables:
        @pl.when(z == owner)
        def _(items=items):
            for slot, (kind, src, dst) in enumerate(items):
                def send(d, carry, kind=kind, src=src, dst=dst, slot=slot):
                    table_copy(kind, src, dst, slot, d).start()
                    return carry
                lax.fori_loop(1, DEEP, send, 0)
                dst[...] = src[...]

    def wait_table(index, item):
        owner, items = tables[index]
        kind, src, dst = items[item]

        @pl.when(z != owner)
        def _():
            table_copy(kind, src, dst, item, 1).wait_recv()

    halos = []

    def swap(src, dst, there):
        index = len(halos)
        copy = pltpu.make_async_remote_copy(
            src_ref=src, dst_ref=dst, send_sem=halo_send.at[index], recv_sem=halo_recv.at[index],
            device_id={"rows": there}, device_id_type=MESH,
        )
        copy.start()
        halos.append(copy)
        return copy

    own = c512[64:576, :]
    c256[64:192, :] = dot(eu[:, 0:256], own[:256]).astype(BF)
    c256[192:320, :] = dot(eu[:, 256:512], own[256:]).astype(BF)
    c128[64:192, :] = dot(eu[:, 512:768], c256[64:320, :]).astype(BF)
    mine64 = dot(eu[:64, 768:896], c128[64:192, :]).astype(BF)
    c64[0] = mine64[:, :HALF]
    c64[1] = mine64[:, HALF:]
    rows_mine = pl.ds(64 + 64 * c, 64)
    rows_theirs = pl.ds(128 - 64 * c, 64)
    to_partner = swap(c64.at[1 - c], n64.at[rows_mine], partner)
    n64[rows_mine, :] = c64[c]

    leaf_left = swap(xs.at[pl.ds(LEAF, LEAF)], xs.at[pl.ds(17 * LEAF, LEAF)], left)
    leaf_right = swap(xs.at[pl.ds(16 * LEAF, LEAF)], xs.at[pl.ds(0, LEAF)], right)
    level_halos = []
    for held, count in ((c128, 4), (c256, 8), (c512, 16)):
        rows = count * RANK
        level_halos.append((
            swap(held.at[pl.ds(64, 64)], held.at[pl.ds(64 + rows, 64)], left),
            swap(held.at[pl.ds(rows, 64)], held.at[pl.ds(0, 64)], right),
        ))

    get_nb.wait()

    def near_leaf(t, carry):
        blocks = []
        for wanted in (-1, 0, 1):
            target = (r * LPD + t + wanted) & 511
            slot = jnp.where(near_list[2, t] == target, 2, jnp.where(near_list[1, t] == target, 1, 0))
            blocks.append(nb[t, slot])
        rows = xs[pl.ds(pl.multiple_of(t * LEAF, LEAF), 3 * LEAF), :]
        near[pl.ds(pl.multiple_of(t * LEAF, LEAF), LEAF), :] = dot(jnp.concatenate(blocks, axis=1), rows).astype(BF)
        return carry

    lax.fori_loop(1, 1 + NEAR_FIRST, near_leaf, 0)
    stores = []

    def store(first, count):
        rows = pl.ds(first * LEAF, count * LEAF)
        copy = pltpu.make_async_copy(near.at[rows], near_out.at[rows], store_sem.at[len(stores)])
        copy.start()
        stores.append(copy)

    to_partner.wait_recv()
    wait_table(0, 0)
    children = iota((128, 128), 0) // RANK
    lanes = iota((128, 128), 1) // RANK
    packed = re64[...].astype(F32)
    eb64 = jnp.where(lanes == 2 * (k % 2) + children // 2, jnp.concatenate([packed, packed], axis=0), 0.0).astype(BF)
    up = dot_t(eb64, n64[64:192, :])
    n32[64:128, :] = (up[:64] + up[64:]).astype(BF)
    wait_table(1, 0)
    eb32 = jnp.where(iota((64, 128), 1) // RANK == k % 4, re32[...].astype(F32), 0.0).astype(BF)
    up = dot_t(eb32, n32[64:128, :])
    c16[k] = (up[:32] + up[32:64] + up[64:96] + up[96:]).astype(BF)

    def ring_copy(src_chip, there, d):
        return pltpu.make_async_remote_copy(
            src_ref=c16.at[src_chip], dst_ref=c16.at[src_chip],
            send_sem=ring_send.at[d], recv_sem=ring_recv.at[src_chip],
            device_id={"rows": there * 2 + c}, device_id_type=MESH,
        )

    def ring_start(d, carry):
        ring_copy(k, (k + d) % CHIPS, d).start()
        return carry

    lax.fori_loop(1, CHIPS, ring_start, 0)
    halos64 = (
        swap(n64.at[pl.ds(64, 64)], n64.at[pl.ds(192, 64)], left2),
        swap(n64.at[pl.ds(128, 64)], n64.at[pl.ds(0, 64)], right2),
    )
    halos32 = (
        swap(n32.at[pl.ds(64, 64)], n32.at[pl.ds(128, 64)], left2),
        swap(n32.at[pl.ds(64, 64)], n32.at[pl.ds(0, 64)], right2),
    )

    get_cf.wait()
    for part in range(7):
        wide_s = dot(cf[4 * part : 4 * part + 4].reshape(4 * 3 * RANK, RANK), spread)
        size, first = ((512, 0), (256, 16), (128, 24))[0 if part < 4 else 1 if part < 6 else 2]
        for i in range(4):
            row = 4 * part + i
            j = r * (size // ROWS) + row - first
            fars = [far_fine[slot, row] for slot in range(3)]
            block = routed(wide_s[i * 3 * RANK : (i + 1) * 3 * RANK], fars, j - row % 2 - 2, size)
            s4[row * RANK : (row + 1) * RANK, :] = block.astype(BF)

    for (from_left, from_right), held, count, first, out in (
        (level_halos[0], c128, 4, 24, g128), (level_halos[1], c256, 8, 16, g256), (level_halos[2], c512, 16, 0, g512),
    ):
        from_left.wait_recv()
        from_right.wait_recv()
        for pair in range(count // 2):
            window = jnp.concatenate([held[64 * pair : 64 * pair + 64, :], held[64 * pair + 128 : 64 * pair + 192, :]], axis=0)
            blocks = s4[first * RANK + 64 * pair : first * RANK + 64 * pair + 64, :]
            out[64 * pair : 64 * pair + 64, :] = dot(blocks, window)

    store(1, NEAR_FIRST)
    lax.fori_loop(1 + NEAR_FIRST, 15, near_leaf, 0)
    leaf_left.wait_recv()
    leaf_right.wait_recv()
    near_leaf(0, 0)
    near_leaf(15, 0)
    store(1 + NEAR_FIRST, 14 - NEAR_FIRST)

    for copies, held, table, blocks, out, pairs in (
        (halos64, n64, 0, rs64, g64, 2), (halos32, n32, 1, rs32, g32, 1),
    ):
        for copy in copies:
            copy.wait_recv()
        wait_table(table, 1)
        for pair in range(pairs):
            window = jnp.concatenate([held[64 * pair : 64 * pair + 64, :], held[64 * pair + 128 : 64 * pair + 192, :]], axis=0)
            out[64 * pair : 64 * pair + 64, :] = dot(blocks[64 * pair : 64 * pair + 64, :], window)

    store(0, 1)
    store(15, 1)

    for item in range(2):
        wait_table(2, item)
    for item in range(3):
        wait_table(3, item)
    mask8 = iota((256, 128), 1) // RANK == iota((256, 128), 0) // 64
    def eight(block):
        wide = block.astype(F32)
        return jnp.where(mask8, jnp.concatenate([wide] * 4, axis=0), 0.0).astype(BF)

    def own_child(block, odd, parent):
        even_rows, odd_rows = block[:RANK].astype(F32), block[RANK:].astype(F32)
        rows = jnp.where(odd == 1, odd_rows, even_rows)
        return jnp.where(iota((RANK, 128), 1) // RANK == parent, rows, 0.0).astype(BF)

    e16 = [eight(re16[0]), eight(re16[1])]
    e8 = eight(re8[...])
    e16_own = own_child(re16[k // 8], k % 2, (k % 8) // 2)
    e8_own = own_child(re8[...], (k // 2) % 2, k // 4)

    def ring_wait(d, carry):
        ring_copy((k + d) % CHIPS, k, d).wait_recv()
        return carry

    lax.fori_loop(1, CHIPS, ring_wait, 0)
    p16 = k // 2
    for group in range(2):
        up = dot_t(e16[group], c16[8 * group : 8 * group + 8].reshape(256, HALF)).astype(BF)
        c8[2 * group] = up[:64]
        c8[2 * group + 1] = up[64:]
    p8 = k // 4
    all8 = c8[...].reshape(256, HALF)
    up = dot_t(e8, all8).astype(BF)
    for j in range(4):
        c4[j] = up[RANK * j : RANK * (j + 1)]
    window = jnp.concatenate(
        [c16[pl.ds(2 * ((p16 + 7) % 8), 2)].reshape(64, HALF), c16[pl.ds(2 * ((p16 + 1) % 8), 2)].reshape(64, HALF)], axis=0
    )
    g16 = dot(rs16[...], window)
    g8 = dot(rs8[...], jnp.concatenate([c8[(p8 + 3) % 4], c8[(p8 + 1) % 4]], axis=0))
    f4 = dot(rs4[:, :RANK], c4[(k // 4 + 2) % 4]).astype(BF)
    f8 = (g8 + dot(e8_own, jnp.concatenate([f4] * 4, axis=0))).astype(BF)
    f16 = (g16 + dot(e16_own, jnp.concatenate([f8] * 4, axis=0))).astype(BF)

    f32_ = (g32[...] + dot(eb32, jnp.concatenate([f16] * 4, axis=0))).astype(BF)
    f64_ = (g64[...] + dot(eb64, jnp.concatenate([f32_] * 2, axis=0))).astype(BF)
    f64[0] = f64_[:64]
    f64[1] = f64_[64:]
    back = swap(f64.at[1 - c], f64.at[2 + c], partner)
    f64[2 + c] = f64[c]
    back.wait_recv()
    parents = jnp.concatenate([f64[2], f64[3]], axis=1)
    f128 = (g128[...] + dot(eb[768:896, :64], parents)).astype(BF)
    f256 = (g256[...] + dot(eb[512:768, :], f128)).astype(BF)
    for group in range(2):
        rows = slice(256 * group, 256 * group + 256)
        moments_out[rows, :] = (g512[rows, :] + dot(eb[rows, :], f256[128 * group : 128 * group + 128])).astype(BF)

    for copy in halos:
        copy.wait_send()
    for copy in stores:
        copy.wait()

    def ring_sent(d, carry):
        ring_copy(k, (k + d) % CHIPS, d).wait_send()
        return carry

    lax.fori_loop(1, CHIPS, ring_sent, 0)
    for owner, items in tables:
        @pl.when(z == owner)
        def _(items=items):
            for slot, (kind, src, dst) in enumerate(items):
                def sent(d, carry, kind=kind, src=src, dst=dst, slot=slot):
                    table_copy(kind, src, dst, slot, d).wait_send()
                    return carry
                lax.fori_loop(1, DEEP, sent, 0)


def tree(near_list, far_fine, far_coarse, sources, near_blocks, basis, transfer_fine, couple_fine, transfer_coarse, couple_coarse):
    smem = pl.BlockSpec(memory_space=pltpu.SMEM)
    hbm = pl.BlockSpec(memory_space=pl.ANY)
    vmem = pl.BlockSpec(memory_space=pltpu.VMEM)
    V = pltpu.VMEM
    dma = pltpu.SemaphoreType.DMA
    scratch = [
        V((4096, WIDE), BF),
        V((18 * LEAF, WIDE), BF), V((16, 3, LEAF, LEAF), BF), V((16, RANK, LEAF), BF), V((28, RANK, RANK), BF),
        V((28, 3, RANK, RANK), BF), V((16, RANK, RANK), BF), V((16, 3, RANK, RANK), BF),
        V((896, 128), BF), V((128, 896), BF), V((896, 128), BF),
        V((640, WIDE), BF), V((384, WIDE), BF), V((256, WIDE), BF), V((2, 64, HALF), BF),
        V((256, HALF), BF), V((192, HALF), BF), V((16, RANK, HALF), BF), V((4, 64, HALF), BF), V((4, RANK, HALF), BF),
        V((4, 64, HALF), BF),
        V((512, WIDE), F32), V((256, WIDE), F32), V((128, WIDE), F32), V((128, HALF), F32), V((64, HALF), F32),
        V((2, 64, 128), BF), V((512, 128), BF), V((64, 128), BF), V((64, 128), BF), V((2, 64, 128), BF), V((64, 128), BF),
        V((128, 128), BF), V((64, 128), BF), V((32, 128), BF), V((32, 128), BF), V((32, 128), BF),
        dma((10,)), dma((4,)), dma((3, DEEP)), dma((9,)), dma((14,)), dma((14,)), dma((CHIPS,)), dma((CHIPS,)),
    ]
    return pl.pallas_call(
        tree_kernel,
        name="tree",
        out_shape=(jax.ShapeDtypeStruct((512, WIDE), BF), jax.ShapeDtypeStruct((4096, WIDE), BF)),
        in_specs=[smem] * 3 + [hbm] * 7,
        out_specs=(vmem, hbm),
        scratch_shapes=scratch,
        compiler_params=pltpu.CompilerParams(
            collective_id=0, has_side_effects=True, vmem_limit_bytes=67043328
        ),
    )(near_list, far_fine, far_coarse, sources, near_blocks, basis, transfer_fine, couple_fine, transfer_coarse, couple_coarse)


def join_kernel(near, basis, moments, out):
    for i in range(2):
        rows = slice(LEAF * i, LEAF * (i + 1))
        far = dot_t(basis[i], moments[RANK * i : RANK * (i + 1), :])
        out[rows, :] = (near[rows, :].astype(F32) + far).astype(BF)


def join(near, basis, moments):
    return pl.pallas_call(
        join_kernel,
        name="join",
        grid=(8,),
        out_shape=jax.ShapeDtypeStruct((4096, WIDE), BF),
        in_specs=[
            pl.BlockSpec((512, WIDE), lambda i: (i, 0)),
            pl.BlockSpec((2, RANK, LEAF), lambda i: (i, 0, 0)),
            pl.BlockSpec((64, WIDE), lambda i: (i, 0)),
        ],
        out_specs=pl.BlockSpec((512, WIDE), lambda i: (i, 0)),
    )(near, basis, moments)


def body(
    sources, near_blocks, near_list, source_basis, target_basis, transfer_fine, transfer_coarse,
    couple_fine, couple_coarse, far_fine, far_coarse,
):
    moments, near = tree(
        near_list.T, far_fine.T, far_coarse.T, sources, near_blocks, jnp.swapaxes(source_basis, 1, 2),
        transfer_fine, couple_fine, transfer_coarse, couple_coarse,
    )
    return join(near, jnp.swapaxes(target_basis, 1, 2), moments)


def solution(mesh):
    in_specs = (
        P("rows", "rhs"), P("rows", None, None, None), P("rows", None), P("rows", None, None), P("rows", None, None),
        P("rows", None, None), P("rhs", None, None), P("rows", None, None, None), P("rhs", None, None, None),
        P("rows", None), P(),
    )
    return jax.shard_map(body, mesh=mesh, in_specs=in_specs, out_specs=P("rows", "rhs"), check_vma=False)
```

time: 170 us -> 37.6 us (0.22)
  matrix products: 77.7 us -> 0 us
  local copies, waits for them, and re-layouts: 44.4 us -> 0 us
  Pallas kernels: 0 us -> 37.3 us
  starting transfers between devices: 32 us -> 0 us
  other arithmetic: 9.4 us -> 0 us
  waiting for transfers between devices: 4.21 us -> 0 us
    dot_general x35 -> x0, matrix products: 77.7 us -> none  [the longest x3 32.6 us: body(): jnp.einsum('npq,nqr->npr', chosen, shifted, preferred_element_type=jnp.fl...]
    pallas_call x0 -> x2, Pallas kernels: none -> 37.3 us  [the longest x1 29.6 us: tree(): pl.pallas_call(tree_kernel, name='tree', out_shape=(jax.ShapeDtypeStruct(...]
    slice x24 -> x0, local copies, waits for them, and re-layouts: 28.4 us -> none  [the longest x11 17.8 us: coarse_pass(): couple_all[clusters:2 * clusters]]
    all_to_all x3 -> x0, starting transfers between devices: 21.6 us -> none  [the longest x1 8.54 us: body(): lax.all_to_all(moments, 'rows', split_axis=2, concat_axis=0, tiled=True)]
    ppermute x8 -> x0, starting transfers between devices: 10.4 us -> none  [the longest x4 5.41 us: padded_2(): lax.ppermute(tail, axis, [(i, (i + 1) % count) for i in range(count)])]
    gather x5 -> x0, local copies, waits for them, and re-layouts: 7.19 us -> none  [couple_masked(): picked = moments[jnp.maximum(partners, 0)]]
    all_to_all x3 -> x0, waiting for transfers between devices: 4.19 us -> none  [the longest x1 4.19 us: from_everyone(): return lax.all_to_all(copies, axis, split_axis=0, concat_axis=0, tiled=True)]
    concatenate x2 -> x0, other arithmetic: 3.64 us -> none  [the longest x1 3.63 us: padded_2(): jnp.concatenate([lax.ppermute(tail, axis, [(i, (i + 1) % count) for i in...]
  transfers between devices with their start and end apart: 11 -> 0, of which waited for: 1 -> 0; matrix products, arithmetic and copies ran while one was open for 34% -> 0% of each run, Pallas kernels for 0% -> 0%
where the time goes in v1:
time: 37.6 us; the launch traced here: 37.3 us
  Pallas kernels  37.3 us (99%)
    pallas_call x1, Pallas kernels, tree(): pl.pallas_call(tree_kernel, name='tree', out_shape=(jax.ShapeDtypeStruct(...  29.6 us
    pallas_call x1, Pallas kernels, join(): pl.pallas_call(join_kernel, name='join', grid=(8,), out_shape=jax.ShapeDt...  7.66 us

profile of v1, /device:TPU:1, one launch (start us, length us, event | category | flops | bytes accessed | tf_op | source)
XLA Modules:
  0.0 37.3 jit_solution(5696029826223472495)
XLA Ops:
  0.0 29.6 %tree.1 = (bf16[512,512]{1,0:T(8,128)(2,1)}, bf16[4096,512]{1,0:T(8,128)(2,1)}) custom-call(s32[3,16]{1,0:T(4,128)} %bitcast.7, s32[3,28]{1,0:T(4,128)} %bitcast.8, s32[3,128]{1,0:T(4,128)} %bitcast.9, bf16[4096,512]{1,0:T(8,128)(2,1)} %sources.1, bf16[16,3,256,256]{3,2,1,0:T(8,128)(2,1)} %near_blocks.1, bf16[16,32,256]{2,1,0:T(8,128)(2,1)} %bitcast.5, ...), custom_call_target="tpu_custom_call" | custom-call | tf_op jit(solution)/shard_map/tree/pallas_call | solution.py:410
  29.7 7.7 %join.1 = bf16[4096,512]{1,0:T(8,128)(2,1)} custom-call(bf16[4096,512]{1,0:T(8,128)(2,1)} %get-tuple-element.7.near, bf16[16,32,256]{2,1,0:T(8,128)(2,1)} %bitcast.6, bf16[512,512]{1,0:T(8,128)(2,1)} %get-tuple-element.8.moments), custom_call_target="tpu_custom_call" | custom-call | tf_op jit(solution)/shard_map/join/pallas_call | solution.py:431

commit v2 on v1

--- a/solution.py
+++ b/solution.py
@@ -11,7 +11,8 @@
 LEAF, RANK, LPD = 256, 32, 16
 ROWS, CHIPS, DEEP = 32, 16, 8
 WIDE, HALF = 512, 256
-NEAR_FIRST = 8
+UNROLL, NEAR_A, NEAR_B = 2, 2, 8
+TREE_VMEM = 50_000_000
 
 
 def dot(a, b):
@@ -45,14 +46,14 @@
 
 
 def tree_kernel(
-    near_list, far_fine, far_coarse,
+    near_list_in, far_fine_in, far_coarse_in,
     sources, near_blocks, basis, transfer_fine, couple_fine, transfer_coarse, couple_coarse,
-    moments_out, near_out,
-    near, xs, nb, sb, tf, cf, tc, cc,
+    moments_out, near,
+    near_list, far_fine, far_coarse, xs, nb, sb, tf, cf, tc, cc,
     eb, eu, s4, c512, c256, c128, c64, n64, n32, c16, c8, c4, f64,
     g512, g256, g128, g64, g32,
     se, ss, re64, re32, re16, re8, rs64, rs32, rs16, rs8, rs4,
-    load_sem, store_sem, tab_send, tab_recv, halo_send, halo_recv, ring_send, ring_recv,
+    load_sem, tab_send, tab_recv, halo_send, halo_recv, ring_send, ring_recv,
 ):
     r = lax.axis_index("rows")
     z = lax.axis_index("rhs")
@@ -90,6 +91,7 @@
 
     get_tc = load(transfer_coarse, tc)
     get_cc = load(couple_coarse, cc)
+    get_far = load(far_coarse_in, far_coarse)
     get_tf = load(transfer_fine, tf)
     get_sb = load(basis, sb)
     chunk = 4 * LEAF
@@ -97,6 +99,8 @@
         load(sources.at[pl.ds(i * chunk, chunk)], xs.at[pl.ds(LEAF + i * chunk, chunk)]) for i in range(4)
     ]
     get_cf = load(couple_fine, cf)
+    get_far_fine = load(far_fine_in, far_fine)
+    get_near_list = load(near_list_in, near_list)
     get_nb = load(near_blocks, nb)
 
     spread = jnp.where(iota((RANK, 128), 1) % RANK == iota((RANK, 128), 0), 1.0, 0.0).astype(BF)
@@ -113,6 +117,7 @@
                 total = total + jnp.where(lane_block == parent, wide_e[row : row + RANK], 0.0)
             se[group, odd * RANK : (odd + 1) * RANK, :] = total.astype(BF)
     get_cc.wait()
+    get_far.wait()
     for quarter in range(4):
         wide_s = dot(cc[4 * quarter : 4 * quarter + 4].reshape(4 * 3 * RANK, RANK), spread)
         first_size = {0: 4, 1: 4, 2: 8, 3: 8}[quarter]
@@ -162,15 +167,21 @@
         (1, [(4, se, re16), (5, ss.at[rows16], rs16)]),
         (0, [(6, se.at[1], re8), (7, ss.at[rows8], rs8), (8, ss.at[rows4], rs4)]),
     ]
-    for owner, items in tables:
+    def send_table(index, item):
+        owner, items = tables[index]
+        kind, src, dst = items[item]
+
         @pl.when(z == owner)
-        def _(items=items):
-            for slot, (kind, src, dst) in enumerate(items):
-                def send(d, carry, kind=kind, src=src, dst=dst, slot=slot):
-                    table_copy(kind, src, dst, slot, d).start()
-                    return carry
-                lax.fori_loop(1, DEEP, send, 0)
-                dst[...] = src[...]
+        def _():
+            def send(d, carry):
+                table_copy(kind, src, dst, item, d).start()
+                return carry
+
+            lax.fori_loop(1, DEEP, send, 0)
+            dst[...] = src[...]
+
+    send_table(0, 0)
+    send_table(1, 0)
 
     def wait_table(index, item):
         owner, items = tables[index]
@@ -204,8 +215,6 @@
     to_partner = swap(c64.at[1 - c], n64.at[rows_mine], partner)
     n64[rows_mine, :] = c64[c]
 
-    leaf_left = swap(xs.at[pl.ds(LEAF, LEAF)], xs.at[pl.ds(17 * LEAF, LEAF)], left)
-    leaf_right = swap(xs.at[pl.ds(16 * LEAF, LEAF)], xs.at[pl.ds(0, LEAF)], right)
     level_halos = []
     for held, count in ((c128, 4), (c256, 8), (c512, 16)):
         rows = count * RANK
@@ -213,7 +222,24 @@
             swap(held.at[pl.ds(64, 64)], held.at[pl.ds(64 + rows, 64)], left),
             swap(held.at[pl.ds(rows, 64)], held.at[pl.ds(0, 64)], right),
         ))
-
+    leaf_left = swap(xs.at[pl.ds(LEAF, LEAF)], xs.at[pl.ds(17 * LEAF, LEAF)], left)
+    leaf_right = swap(xs.at[pl.ds(16 * LEAF, LEAF)], xs.at[pl.ds(0, LEAF)], right)
+    for index, item in ((2, 0), (3, 0), (0, 1), (1, 1), (2, 1), (3, 1), (3, 2)):
+        send_table(index, item)
+
+    get_cf.wait()
+    get_far_fine.wait()
+    for part in range(7):
+        wide_s = dot(cf[4 * part : 4 * part + 4].reshape(4 * 3 * RANK, RANK), spread)
+        size, first = ((512, 0), (256, 16), (128, 24))[0 if part < 4 else 1 if part < 6 else 2]
+        for i in range(4):
+            row = 4 * part + i
+            j = r * (size // ROWS) + row - first
+            fars = [far_fine[slot, row] for slot in range(3)]
+            block = routed(wide_s[i * 3 * RANK : (i + 1) * 3 * RANK], fars, j - row % 2 - 2, size)
+            s4[row * RANK : (row + 1) * RANK, :] = block.astype(BF)
+
+    get_near_list.wait()
     get_nb.wait()
 
     def near_leaf(t, carry):
@@ -226,16 +252,22 @@
         near[pl.ds(pl.multiple_of(t * LEAF, LEAF), LEAF), :] = dot(jnp.concatenate(blocks, axis=1), rows).astype(BF)
         return carry
 
-    lax.fori_loop(1, 1 + NEAR_FIRST, near_leaf, 0)
-    stores = []
-
-    def store(first, count):
-        rows = pl.ds(first * LEAF, count * LEAF)
-        copy = pltpu.make_async_copy(near.at[rows], near_out.at[rows], store_sem.at[len(stores)])
-        copy.start()
-        stores.append(copy)
+    def near_leaves(first, count):
+        def some(i, carry):
+            for u in range(UNROLL):
+                near_leaf(first + i * UNROLL + u, 0)
+            return carry
+
+        lax.fori_loop(0, count // UNROLL, some, 0)
+
+    near_leaves(1, NEAR_A)
 
     to_partner.wait_recv()
+    halos64 = (
+        swap(n64.at[pl.ds(64, 64)], n64.at[pl.ds(192, 64)], left2),
+        swap(n64.at[pl.ds(128, 64)], n64.at[pl.ds(0, 64)], right2),
+    )
+    near_leaves(1 + NEAR_A, NEAR_B)
     wait_table(0, 0)
     children = iota((128, 128), 0) // RANK
     lanes = iota((128, 128), 1) // RANK
@@ -260,25 +292,10 @@
         return carry
 
     lax.fori_loop(1, CHIPS, ring_start, 0)
-    halos64 = (
-        swap(n64.at[pl.ds(64, 64)], n64.at[pl.ds(192, 64)], left2),
-        swap(n64.at[pl.ds(128, 64)], n64.at[pl.ds(0, 64)], right2),
-    )
     halos32 = (
         swap(n32.at[pl.ds(64, 64)], n32.at[pl.ds(128, 64)], left2),
         swap(n32.at[pl.ds(64, 64)], n32.at[pl.ds(0, 64)], right2),
     )
-
-    get_cf.wait()
-    for part in range(7):
-        wide_s = dot(cf[4 * part : 4 * part + 4].reshape(4 * 3 * RANK, RANK), spread)
-        size, first = ((512, 0), (256, 16), (128, 24))[0 if part < 4 else 1 if part < 6 else 2]
-        for i in range(4):
-            row = 4 * part + i
-            j = r * (size // ROWS) + row - first
-            fars = [far_fine[slot, row] for slot in range(3)]
-            block = routed(wide_s[i * 3 * RANK : (i + 1) * 3 * RANK], fars, j - row % 2 - 2, size)
-            s4[row * RANK : (row + 1) * RANK, :] = block.astype(BF)
 
     for (from_left, from_right), held, count, first, out in (
         (level_halos[0], c128, 4, 24, g128), (level_halos[1], c256, 8, 16, g256), (level_halos[2], c512, 16, 0, g512),
@@ -290,17 +307,13 @@
             blocks = s4[first * RANK + 64 * pair : first * RANK + 64 * pair + 64, :]
             out[64 * pair : 64 * pair + 64, :] = dot(blocks, window)
 
-    store(1, NEAR_FIRST)
-    lax.fori_loop(1 + NEAR_FIRST, 15, near_leaf, 0)
+    near_leaves(1 + NEAR_A + NEAR_B, 14 - NEAR_A - NEAR_B)
     leaf_left.wait_recv()
     leaf_right.wait_recv()
     near_leaf(0, 0)
     near_leaf(15, 0)
-    store(1 + NEAR_FIRST, 14 - NEAR_FIRST)
-
-    for copies, held, table, blocks, out, pairs in (
-        (halos64, n64, 0, rs64, g64, 2), (halos32, n32, 1, rs32, g32, 1),
-    ):
+
+    def couple_chip(copies, held, table, blocks, out, pairs):
         for copy in copies:
             copy.wait_recv()
         wait_table(table, 1)
@@ -308,8 +321,7 @@
             window = jnp.concatenate([held[64 * pair : 64 * pair + 64, :], held[64 * pair + 128 : 64 * pair + 192, :]], axis=0)
             out[64 * pair : 64 * pair + 64, :] = dot(blocks[64 * pair : 64 * pair + 64, :], window)
 
-    store(0, 1)
-    store(15, 1)
+    couple_chip(halos64, n64, 0, rs64, g64, 2)
 
     for item in range(2):
         wait_table(2, item)
@@ -333,6 +345,15 @@
     def ring_wait(d, carry):
         ring_copy((k + d) % CHIPS, k, d).wait_recv()
         return carry
+
+    for owner, items in tables:
+        @pl.when(z == owner)
+        def _(items=items):
+            for slot, (kind, src, dst) in enumerate(items):
+                def sent(d, carry, kind=kind, src=src, dst=dst, slot=slot):
+                    table_copy(kind, src, dst, slot, d).wait_send()
+                    return carry
+                lax.fori_loop(1, DEEP, sent, 0)
 
     lax.fori_loop(1, CHIPS, ring_wait, 0)
     p16 = k // 2
@@ -354,12 +375,21 @@
     f8 = (g8 + dot(e8_own, jnp.concatenate([f4] * 4, axis=0))).astype(BF)
     f16 = (g16 + dot(e16_own, jnp.concatenate([f8] * 4, axis=0))).astype(BF)
 
+    couple_chip(halos32, n32, 1, rs32, g32, 1)
     f32_ = (g32[...] + dot(eb32, jnp.concatenate([f16] * 4, axis=0))).astype(BF)
     f64_ = (g64[...] + dot(eb64, jnp.concatenate([f32_] * 2, axis=0))).astype(BF)
     f64[0] = f64_[:64]
     f64[1] = f64_[64:]
     back = swap(f64.at[1 - c], f64.at[2 + c], partner)
     f64[2 + c] = f64[c]
+
+    def ring_sent(d, carry):
+        ring_copy(k, (k + d) % CHIPS, d).wait_send()
+        return carry
+
+    lax.fori_loop(1, CHIPS, ring_sent, 0)
+    for copy in halos:
+        copy.wait_send()
     back.wait_recv()
     parents = jnp.concatenate([f64[2], f64[3]], axis=1)
     f128 = (g128[...] + dot(eb[768:896, :64], parents)).astype(BF)
@@ -368,34 +398,15 @@
         rows = slice(256 * group, 256 * group + 256)
         moments_out[rows, :] = (g512[rows, :] + dot(eb[rows, :], f256[128 * group : 128 * group + 128])).astype(BF)
 
-    for copy in halos:
-        copy.wait_send()
-    for copy in stores:
-        copy.wait()
-
-    def ring_sent(d, carry):
-        ring_copy(k, (k + d) % CHIPS, d).wait_send()
-        return carry
-
-    lax.fori_loop(1, CHIPS, ring_sent, 0)
-    for owner, items in tables:
-        @pl.when(z == owner)
-        def _(items=items):
-            for slot, (kind, src, dst) in enumerate(items):
-                def sent(d, carry, kind=kind, src=src, dst=dst, slot=slot):
-                    table_copy(kind, src, dst, slot, d).wait_send()
-                    return carry
-                lax.fori_loop(1, DEEP, sent, 0)
-
 
 def tree(near_list, far_fine, far_coarse, sources, near_blocks, basis, transfer_fine, couple_fine, transfer_coarse, couple_coarse):
-    smem = pl.BlockSpec(memory_space=pltpu.SMEM)
     hbm = pl.BlockSpec(memory_space=pl.ANY)
     vmem = pl.BlockSpec(memory_space=pltpu.VMEM)
     V = pltpu.VMEM
     dma = pltpu.SemaphoreType.DMA
+    S = pltpu.SMEM
     scratch = [
-        V((4096, WIDE), BF),
+        S((3, 16), jnp.int32), S((3, 28), jnp.int32), S((3, 128), jnp.int32),
         V((18 * LEAF, WIDE), BF), V((16, 3, LEAF, LEAF), BF), V((16, RANK, LEAF), BF), V((28, RANK, RANK), BF),
         V((28, 3, RANK, RANK), BF), V((16, RANK, RANK), BF), V((16, 3, RANK, RANK), BF),
         V((896, 128), BF), V((128, 896), BF), V((896, 128), BF),
@@ -405,40 +416,50 @@
         V((512, WIDE), F32), V((256, WIDE), F32), V((128, WIDE), F32), V((128, HALF), F32), V((64, HALF), F32),
         V((2, 64, 128), BF), V((512, 128), BF), V((64, 128), BF), V((64, 128), BF), V((2, 64, 128), BF), V((64, 128), BF),
         V((128, 128), BF), V((64, 128), BF), V((32, 128), BF), V((32, 128), BF), V((32, 128), BF),
-        dma((10,)), dma((4,)), dma((3, DEEP)), dma((9,)), dma((14,)), dma((14,)), dma((CHIPS,)), dma((CHIPS,)),
+        dma((16,)), dma((3, DEEP)), dma((9,)), dma((14,)), dma((14,)), dma((CHIPS,)), dma((CHIPS,)),
     ]
     return pl.pallas_call(
         tree_kernel,
         name="tree",
         out_shape=(jax.ShapeDtypeStruct((512, WIDE), BF), jax.ShapeDtypeStruct((4096, WIDE), BF)),
-        in_specs=[smem] * 3 + [hbm] * 7,
-        out_specs=(vmem, hbm),
+        in_specs=[hbm] * 10,
+        out_specs=(vmem, vmem),
         scratch_shapes=scratch,
         compiler_params=pltpu.CompilerParams(
-            collective_id=0, has_side_effects=True, vmem_limit_bytes=67043328
+            collective_id=0, has_side_effects=True, vmem_limit_bytes=TREE_VMEM
         ),
-    )(near_list, far_fine, far_coarse, sources, near_blocks, basis, transfer_fine, couple_fine, transfer_coarse, couple_coarse)
-
-
-def join_kernel(near, basis, moments, out):
-    for i in range(2):
-        rows = slice(LEAF * i, LEAF * (i + 1))
-        far = dot_t(basis[i], moments[RANK * i : RANK * (i + 1), :])
-        out[rows, :] = (near[rows, :].astype(F32) + far).astype(BF)
+    )(*(pltpu.with_memory_space_constraint(x, pltpu.HBM) for x in (
+        near_list, far_fine, far_coarse, sources, near_blocks, basis, transfer_fine, couple_fine, transfer_coarse, couple_coarse
+    )))
+
+
+def join_kernel(near, basis, moments, out, held, out_sem):
+    copies = []
+    for t in range(LPD):
+        rows = pl.ds(LEAF * t, LEAF)
+        far = dot_t(basis[t], moments[RANK * t : RANK * (t + 1), :])
+        held[rows, :] = (near[rows, :].astype(F32) + far).astype(BF)
+        if t % 2:
+            both = pl.ds(LEAF * (t - 1), 2 * LEAF)
+            copy = pltpu.make_async_copy(held.at[both], out.at[both], out_sem.at[t // 2])
+            copy.start()
+            copies.append(copy)
+    for copy in copies:
+        copy.wait()
 
 
 def join(near, basis, moments):
+    vmem = pl.BlockSpec(memory_space=pltpu.VMEM)
+    hbm = pl.BlockSpec(memory_space=pl.ANY)
+    dma = pltpu.SemaphoreType.DMA
     return pl.pallas_call(
         join_kernel,
         name="join",
-        grid=(8,),
         out_shape=jax.ShapeDtypeStruct((4096, WIDE), BF),
-        in_specs=[
-            pl.BlockSpec((512, WIDE), lambda i: (i, 0)),
-            pl.BlockSpec((2, RANK, LEAF), lambda i: (i, 0, 0)),
-            pl.BlockSpec((64, WIDE), lambda i: (i, 0)),
-        ],
-        out_specs=pl.BlockSpec((512, WIDE), lambda i: (i, 0)),
+        in_specs=[vmem, vmem, vmem],
+        out_specs=hbm,
+        scratch_shapes=[pltpu.VMEM((4096, WIDE), BF), dma((8,))],
+        compiler_params=pltpu.CompilerParams(vmem_limit_bytes=16 * 1024 * 1024),
     )(near, basis, moments)
 
 

time: 37.6 us -> 29.7 us (0.79)
  Pallas kernels: 37.3 us -> 29.6 us
    pallas_call x1, Pallas kernels: 7.66 us -> 2.39 us  [join(): pl.pallas_call(join_kernel, name='join', out_shape=jax.ShapeDtypeStruct((...]
    pallas_call x1, Pallas kernels: 29.6 us -> 27.2 us  [tree(): pl.pallas_call(tree_kernel, name='tree', out_shape=(jax.ShapeDtypeStruct(...]
where the time goes in v2:
time: 29.7 us
  Pallas kernels  29.6 us (100%)
    pallas_call x1, Pallas kernels, tree(): pl.pallas_call(tree_kernel, name='tree', out_shape=(jax.ShapeDtypeStruct(...  27.2 us
    pallas_call x1, Pallas kernels, join(): pl.pallas_call(join_kernel, name='join', out_shape=jax.ShapeDtypeStruct((...  2.39 us

profile of v2, /device:TPU:1, one launch (start us, length us, event | category | flops | bytes accessed | tf_op | source)
XLA Modules:
  0.0 29.7 jit_solution(1884197034413115230)
XLA Ops:
  0.0 0.0 copy-start
  0.0 27.2 %tree.1 = (bf16[512,512]{1,0:T(8,128)(2,1)S(1)}, bf16[4096,512]{1,0:T(8,128)(2,1)S(1)}) custom-call(s32[3,16]{1,0:T(4,128)} %bitcast.7, s32[3,28]{1,0:T(4,128)} %bitcast.8, s32[3,128]{1,0:T(4,128)} %bitcast.9, bf16[4096,512]{1,0:T(8,128)(2,1)} %sources.1, bf16[16,3,256,256]{3,2,1,0:T(8,128)(2,1)} %near_blocks.1, bf16[16,32,256]{2,1,0:T(8,128)(2,1)} %bitcast.6, ...), custom_call_target="tpu_custom_call" | custom-call | tf_op jit(solution)/shard_map/tree/pallas_call | solution.py:421
  27.3 0.0 copy-done
  27.3 2.4 %join.1 = bf16[4096,512]{1,0:T(8,128)(2,1)} custom-call(bf16[4096,512]{1,0:T(8,128)(2,1)S(1)} %get-tuple-element.7.near, bf16[16,32,256]{2,1,0:T(8,128)(2,1)S(1)} %bitcast.5, bf16[512,512]{1,0:T(8,128)(2,1)S(1)} %get-tuple-element.8.moments), custom_call_target="tpu_custom_call" | custom-call | tf_op jit(solution)/shard_map/join/pallas_call | solution.py:455
Async XLA Ops:
  0.0 27.3 %copy-start = (bf16[16,256,32]{1,2,0:T(8,128)(2,1)S(1)}, bf16[16,256,32]{1,2,0:T(8,128)(2,1)}, u32[]{:S(2)}) copy-start(bf16[16,256,32]{1,2,0:T(8,128)(2,1)} %param.15) | copy-start | bytes 786436
